TPU v7x, 32 devices: a whole 2x2x4 slice. The times are simulated.
32 devices in a mesh: seg: 4 (over y, x), lat: 8 (over z, core).
Axes of the slice: x: 2, y: 2, z: 4, core: 2. Of those that a mesh axis runs over, the one named last changes fastest.
Arguments:
- coh_map: bfloat16 [4, 65536, 128], P('seg', 'lat'), may hold values from 0 to 40, as said below
- positions: int32 [4, 1024], P('seg', 'lat'), may hold values from 0 to 16776959, as said below
- counts: int32 [16], P('lat'), may hold values from 1 to 64, as said below
Outputs:
- semi_stat: bfloat16 [1024, 128], P('lat')
- excess: float32 [16, 128], P('lat')
Inputs may be any that keep to these rules, and one draw needn't show every extreme that they name: `coh_map`: nonnegative. `counts`: the first block has 1 valid point and the last block 64. `positions`: the bins are split into 8 aligned slices of 8192 bins; a point's two bins lie in the same slice; in each segment, at most 32 of the 128 points of one index of lat have their bins in one slice, and that most is reached in every draw.
All inputs are finite; a program needn't handle non-finite values.
Results may differ from a plain program's by a relative error of at most 0.001.
Values sent between devices are 32-bit elements; how exact they have to be, the bound alone decides.
A program may use at most 64 MiB of HBM per device.

v0:
```python
import functools

import jax
import jax.numpy as jnp
from jax import lax
from jax.experimental import pallas as pl
from jax.experimental.pallas import tpu as pltpu
from jax.sharding import PartitionSpec as P

MESH = pl.DeviceIdType.MESH
PIECES = 1
PARTS = 4
CUTS = 2


def flip(index, mask):
    out = index
    w = 1
    while w <= mask:
        if mask & w:
            out = out + w - 2 * w * lax.rem(index // w, 2)
        w *= 2
    return out


def kernel(
    n_lat,
    n_seg,
    pos_hbm,
    cnt_hbm,
    coh_hbm,
    semi_ref,
    excess_ref,
    pos_ref,
    cnt_ref,
    coh,
    gath,
    rows_out,
    rows_in,
    col_out,
    col_in,
    part,
    part_in,
    psum,
    psum_in,
    coh_sem,
    gs_sem,
    gr_sem,
    rs_sem,
    rr_sem,
    cs_sem,
    cr_sem,
    xs_sem,
    xr_sem,
    in_sem,
):
    lat = lax.axis_index("lat")
    seg = lax.axis_index("seg")
    slice_bins, width = coh.shape
    points = pos_ref.shape[1]
    blocks = cnt_ref.shape[0]
    block_size = points // blocks
    slots = 2 * points // n_lat
    total_slots = n_lat * slots
    f32, bf16, i32 = jnp.float32, jnp.bfloat16, jnp.int32

    barrier = pltpu.get_barrier_semaphore()
    lat_peers = [flip(lat, j) for j in range(n_lat)]
    far_first = list(range(n_lat - 1, 0, -1))
    for j in far_first:
        pl.semaphore_signal(barrier, inc=1, device_id=(seg, lat_peers[j]), device_id_type=MESH)
    for b in range(1, n_seg):
        pl.semaphore_signal(barrier, inc=1, device_id=(flip(seg, b), lat), device_id_type=MESH)

    small = [
        pltpu.make_async_copy(pos_hbm, pos_ref, in_sem.at[0]),
        pltpu.make_async_copy(cnt_hbm, cnt_ref, in_sem.at[1]),
    ]
    for copy in small:
        copy.start()
    piece = slice_bins // PIECES
    loads = []
    for k in range(PIECES):
        rng = pl.ds(k * piece, piece)
        loads.append(pltpu.make_async_copy(coh_hbm.at[0, rng], coh.at[rng], coh_sem.at[k]))
        loads[-1].start()
    for copy in small:
        copy.wait()

    pos = pos_ref[...]
    lane = lax.broadcasted_iota(i32, (1, points), 1)
    dest = (pos // 256) // slice_bins
    rel = jnp.bitwise_xor(dest, jnp.full((1, points), lat, i32))
    hits = lax.broadcasted_iota(i32, (n_lat, points), 0) == rel
    hits_f = hits.astype(f32)
    tri = (
        lax.broadcasted_iota(i32, (points, points), 0)
        < lax.broadcasted_iota(i32, (points, points), 1)
    ).astype(f32)
    before = jnp.dot(hits_f.astype(bf16), tri.astype(bf16), preferred_element_type=f32)
    slot = jnp.sum(before * hits_f, axis=0, keepdims=True).astype(i32)
    sid = rel * slots + slot
    limit = jnp.zeros((1, points), i32)
    for b in range(blocks):
        limit = jnp.where(lane // block_size == b, cnt_ref[b], limit)
    valid = (lane % block_size < limit).astype(i32)
    gath[0, 0:1, :] = sid
    gath[0, 1:2, :] = pos
    gath[0, 2:3, :] = valid
    gath[0, 3:4, :] = valid

    pl.semaphore_wait(barrier, n_lat - 1 + n_seg - 1)
    sends = []
    for j in far_first:
        copy = pltpu.make_async_remote_copy(
            src_ref=gath.at[0],
            dst_ref=gath.at[j],
            send_sem=gs_sem.at[j],
            recv_sem=gr_sem.at[j],
            device_id=(seg, lat_peers[j]),
            device_id_type=MESH,
        )
        copy.start()
        sends.append(copy)

    pick_t = (lax.broadcasted_iota(i32, (total_slots, points), 0) == sid).astype(f32)
    pick = pick_t.T.astype(bf16)

    arriving = {j: copy for j, copy in zip(far_first, sends)}

    pos_bits = 8
    bin_bits = (slice_bins - 1).bit_length()
    depth = min(256, slice_bins)
    depth_bits = depth.bit_length() - 1
    base = lat * (slice_bins << pos_bits)
    flag = slice_bins << pos_bits
    sub = lax.broadcasted_iota(i32, (slots, points), 0)
    group = n_lat // PARTS
    span = group * slots
    bins = lax.broadcasted_iota(i32, (span, depth), 1)
    zero = jnp.zeros((span, depth), bf16)
    per_piece = piece // depth
    count = jnp.zeros((1, points), i32)
    col = jnp.zeros((1, width), f32)
    back, col_back = [], []
    coming = {}
    for part_id in range(PARTS):
        owners = list(range(part_id * group, (part_id + 1) * group))
        cols = []
        for j in owners:
            if j > 0:
                arriving[j].wait_recv()
            live_row = gath[j, 2:3, :]
            code = (gath[j, 1:2, :] - base + flag * (1 + live_row)).astype(f32)
            here = (gath[j, 0:1, :] - j * slots) == sub
            cols.append(jnp.sum(jnp.where(here, code, 0.0), axis=1, keepdims=True))
            count = count + live_row
        code = jnp.concatenate(cols, axis=0).astype(i32)
        kind = lax.shift_right_logical(code, bin_bits + pos_bits)
        low = lax.shift_right_logical(code & (flag - 1), pos_bits)
        upper = (code & ((1 << pos_bits) - 1)).astype(f32) * (1.0 / (1 << pos_bits))
        chunk = jnp.where(kind > 0, lax.shift_right_logical(low, depth_bits), -2)
        in_chunk = low & (depth - 1)
        local = jnp.where(bins == in_chunk, 1.0 - upper, 0.0)
        local = jnp.where(bins == ((in_chunk + 1) & (depth - 1)), upper, local).astype(bf16)
        where_id = jnp.where(bins < in_chunk, chunk + 1, chunk).astype(f32).astype(bf16)
        held = jnp.zeros((span, width), f32)
        for k in range(PIECES):
            if part_id == 0:
                loads[k].wait()
            weights = jnp.concatenate(
                [
                    jnp.where(where_id == jnp.asarray(k * per_piece + c, bf16), local, zero)
                    for c in range(per_piece)
                ],
                axis=1,
            )
            held = held + jnp.dot(
                weights, coh[k * piece : (k + 1) * piece, :], preferred_element_type=f32
            )
        for i, j in enumerate(owners):
            rows_out[j] = held[i * slots : (i + 1) * slots, :]
        for j in reversed(owners):
            if j == 0:
                continue
            copy = pltpu.make_async_remote_copy(
                src_ref=rows_out.at[j],
                dst_ref=rows_in.at[j],
                send_sem=rs_sem.at[j],
                recv_sem=rr_sem.at[j],
                device_id=(seg, lat_peers[j]),
                device_id_type=MESH,
            )
            copy.start()
            back.append(copy)
            coming[j] = copy
        col = col + jnp.sum(jnp.where(kind > 1, held, 0.0), axis=0, keepdims=True)
    col_out[...] = col
    for j in far_first:
        copy = pltpu.make_async_remote_copy(
            src_ref=col_out,
            dst_ref=col_in.at[j],
            send_sem=cs_sem.at[j],
            recv_sem=cr_sem.at[j],
            device_id=(seg, lat_peers[j]),
            device_id_type=MESH,
        )
        copy.start()
        col_back.append(copy)
    total_count = jnp.sum(count.astype(f32), axis=1, keepdims=True)

    highs = []
    rests = []
    for part_id in range(PARTS):
        owners = list(range(part_id * group, (part_id + 1) * group))
        got = []
        for j in owners:
            if j > 0:
                coming[j].wait_recv()
            got.append(rows_in[j] if j > 0 else rows_out[0])
        got = jnp.concatenate(got, axis=0)
        high = got.astype(bf16)
        highs.append(high)
        rests.append((got - high.astype(f32)).astype(bf16))
    spread = jnp.concatenate(highs + rests, axis=0)
    outs = []

    def tell(src, dsts, q):
        for m in range(n_seg - 1, 0, -1):
            copy = pltpu.make_async_remote_copy(
                src_ref=src,
                dst_ref=dsts[m],
                send_sem=xs_sem.at[m, q],
                recv_sem=xr_sem.at[m, q],
                device_id=(flip(seg, m), lat),
                device_id_type=MESH,
            )
            copy.start()
            outs.append(copy)

    part_rows = points // CUTS
    for h in range(CUTS):
        rng = pl.ds(h * part_rows, part_rows)
        mine = pick[h * part_rows : (h + 1) * part_rows]
        part[0, rng] = jnp.dot(
            jnp.concatenate([mine, mine], axis=1), spread, preferred_element_type=f32
        )
        tell(part.at[0, rng], [part_in.at[m, rng] for m in range(n_seg)], h)

    def tree(terms):
        w = 1
        while w < n_seg:
            terms = [terms[i] + terms[i + 1] for i in range(0, len(terms), 2)]
            w *= 2
        return terms[0]

    for copy in col_back:
        copy.wait_recv()
    for j in range(1, n_lat):
        col = col + col_in[j]
    psum[0] = col
    tell(psum.at[0], [psum_in.at[m] for m in range(n_seg)], CUTS)
    for copy in outs:
        copy.wait_recv()
    stat = tree([part[0]] + [part_in[m] for m in range(1, n_seg)]) / n_seg
    col = tree([col] + [psum_in[m] for m in range(1, n_seg)])
    semi_ref[...] = stat.astype(semi_ref.dtype)
    global_mean = (col / n_seg) / total_count
    row = lax.broadcasted_iota(i32, (block_size, width), 0)
    for b in range(blocks):
        block = stat[b * block_size : (b + 1) * block_size]
        block_sum = jnp.sum(jnp.where(row < cnt_ref[b], block, 0.0), axis=0, keepdims=True)
        mean = block_sum / jnp.full((1, width), cnt_ref[b], i32).astype(f32)
        excess_ref[b : b + 1, :] = mean - global_mean

    for copy in sends + back + col_back + outs:
        copy.wait_send()


def deliver(semi_ref, excess_ref, semi_out, excess_out, sem):
    copies = [
        pltpu.make_async_copy(semi_ref, semi_out, sem.at[0]),
        pltpu.make_async_copy(excess_ref, excess_out, sem.at[1]),
    ]
    for copy in copies:
        copy.start()
    for copy in copies:
        copy.wait()


def shards(n_lat, n_seg, coh_map, positions, counts):
    _, slice_bins, width = coh_map.shape
    points = positions.shape[1]
    blocks = counts.shape[0]
    slots = 2 * points // n_lat
    f32 = jnp.float32
    dma = pltpu.SemaphoreType.DMA
    made = pl.pallas_call(
        functools.partial(kernel, n_lat, n_seg),
        out_shape=(
            pltpu.VMEM((points, width), jnp.bfloat16),
            pltpu.VMEM((blocks, width), f32),
        ),
        in_specs=[
            pl.BlockSpec(memory_space=pl.ANY),
            pl.BlockSpec(memory_space=pl.ANY),
            pl.BlockSpec(memory_space=pl.ANY),
        ],
        out_specs=(
            pl.BlockSpec(memory_space=pltpu.VMEM),
            pl.BlockSpec(memory_space=pltpu.VMEM),
        ),
        scratch_shapes=[
            pltpu.VMEM((1, points), jnp.int32),
            pltpu.SMEM((blocks,), jnp.int32),
            pltpu.VMEM((slice_bins, width), coh_map.dtype),
            pltpu.VMEM((n_lat, 4, points), jnp.int32),
            pltpu.VMEM((n_lat, slots, width), f32),
            pltpu.VMEM((n_lat, slots, width), f32),
            pltpu.VMEM((1, width), f32),
            pltpu.VMEM((n_lat, 1, width), f32),
            pltpu.VMEM((n_seg, points, width), f32),
            pltpu.VMEM((n_seg, points, width), f32),
            pltpu.VMEM((n_seg, 1, width), f32),
            pltpu.VMEM((n_seg, 1, width), f32),
            dma((PIECES,)),
            dma((n_lat,)),
            dma((n_lat,)),
            dma((n_lat,)),
            dma((n_lat,)),
            dma((n_lat,)),
            dma((n_lat,)),
            dma((n_seg, CUTS + 1)),
            dma((n_seg, CUTS + 1)),
            dma((2,)),
        ],
        compiler_params=pltpu.CompilerParams(collective_id=0, has_side_effects=True),
    )(positions, counts, coh_map)
    made = [pltpu.with_memory_space_constraint(x, pltpu.VMEM) for x in made]
    return pl.pallas_call(
        deliver,
        out_shape=tuple(jax.ShapeDtypeStruct(x.shape, x.dtype) for x in made),
        in_specs=[pl.BlockSpec(memory_space=pltpu.VMEM)] * 2,
        out_specs=(pl.BlockSpec(memory_space=pl.ANY),) * 2,
        scratch_shapes=[dma((2,))],
    )(*made)


def solution(mesh):
    in_specs = (P("seg", "lat", None), P("seg", "lat"), P("lat"))
    out_specs = (P("lat", None), P("lat", None))
    body = functools.partial(shards, mesh.shape["lat"], mesh.shape["seg"])
    return jax.shard_map(body, mesh=mesh, in_specs=in_specs, out_specs=out_specs, check_vma=False)
```

profile of v0, /device:TPU:0, one launch (start us, length us, event | category | flops | bytes accessed | tf_op | source)
XLA Modules:
  0.0 21.5 jit_solution(8880055709680919373)
XLA Ops:
  0.6 20.3 %shard_map.50 = (bf16[128,128]{1,0:T(8,128)(2,1)S(1)}, f32[2,128]{1,0:T(2,128)S(1)}) custom-call(s32[1,128]{1,0:T(1,128)} %pos_hbm.1, s32[2]{0:T(128)} %cnt_hbm.1, bf16[1,8192,128]{2,1,0:T(8,128)(2,1)} %coh_hbm.1), custom_call_target="tpu_custom_call" | custom-call | tf_op jit(solution)/shard_map/pallas_call | solution.py:298
  20.9 0.6 %shard_map.51 = (bf16[128,128]{1,0:T(8,128)(2,1)}, f32[2,128]{1,0:T(2,128)}) custom-call(bf16[128,128]{1,0:T(8,128)(2,1)S(1)} %get-tuple-element.4.semi_ref, f32[2,128]{1,0:T(2,128)S(1)} %get-tuple-element.5.excess_ref), custom_call_target="tpu_custom_call" | custom-call | tf_op jit(solution)/shard_map/pallas_call | solution.py:340
where the time goes:
time: 21.7 us; the launch traced here: 21.5 us
  Pallas kernels  20.9 us (96%)
  between operations  0.64 us (3%)
    pallas_call x1, Pallas kernels, shards(): pl.pallas_call(functools.partial(kernel, n_lat, n_seg), out_shape=(pltpu....  20.3 us
    pallas_call x1, Pallas kernels, shards(): pl.pallas_call(deliver, out_shape=tuple((jax.ShapeDtypeStruct(x.shape, x....  0.64 us

commit v1 on v0

v1 whole, which is shorter than its diff:
```python
import functools

import jax
import jax.numpy as jnp
from jax import lax
from jax.experimental import pallas as pl
from jax.experimental.pallas import tpu as pltpu
from jax.sharding import PartitionSpec as P

MESH = pl.DeviceIdType.MESH
PARTS = 4


def flip(index, mask):
    out = index
    w = 1
    while w <= mask:
        if mask & w:
            out = out + w - 2 * w * lax.rem(index // w, 2)
        w *= 2
    return out


def kernel(
    n_lat,
    n_seg,
    pos_hbm,
    cnt_hbm,
    coh_hbm,
    semi_ref,
    excess_ref,
    pos_ref,
    cnt_ref,
    coh,
    gath,
    rows_out,
    rows_in,
    col_out,
    col_in,
    sid_in,
    far_rows,
    psum,
    psum_in,
    coh_sem,
    gs_sem,
    gr_sem,
    rs_sem,
    rr_sem,
    cs_sem,
    cr_sem,
    xs_sem,
    xr_sem,
    ss_sem,
    sr_sem,
    ps_sem,
    pr_sem,
    in_sem,
):
    lat = lax.axis_index("lat")
    seg = lax.axis_index("seg")
    slice_bins, width = coh.shape
    points = pos_ref.shape[1]
    blocks = cnt_ref.shape[0]
    block_size = points // blocks
    slots = 2 * points // n_lat
    total_slots = n_lat * slots
    f32, bf16, i32 = jnp.float32, jnp.bfloat16, jnp.int32
    group = n_lat // PARTS
    span = group * slots
    quarter = lat // group

    def remote(src, dst, send_sem, recv_sem, to):
        return pltpu.make_async_remote_copy(
            src_ref=src,
            dst_ref=dst,
            send_sem=send_sem,
            recv_sem=recv_sem,
            device_id=to,
            device_id_type=MESH,
        )

    barrier = pltpu.get_barrier_semaphore()
    lat_peers = [flip(lat, j) for j in range(n_lat)]
    seg_peers = [flip(seg, m) for m in range(n_seg)]
    far_first = list(range(n_lat - 1, 0, -1))
    seg_far_first = list(range(n_seg - 1, 0, -1))
    for j in far_first:
        pl.semaphore_signal(barrier, inc=1, device_id=(seg, lat_peers[j]), device_id_type=MESH)
    for m in seg_far_first:
        pl.semaphore_signal(barrier, inc=1, device_id=(seg_peers[m], lat), device_id_type=MESH)

    small = [
        pltpu.make_async_copy(pos_hbm, pos_ref, in_sem.at[0]),
        pltpu.make_async_copy(cnt_hbm, cnt_ref, in_sem.at[1]),
    ]
    for copy in small:
        copy.start()
    load = pltpu.make_async_copy(coh_hbm.at[0], coh, coh_sem)
    load.start()
    for copy in small:
        copy.wait()

    pos = pos_ref[...]
    lane = lax.broadcasted_iota(i32, (1, points), 1)
    dest = (pos // 256) // slice_bins
    rel = jnp.bitwise_xor(dest, jnp.full((1, points), lat, i32))
    hits = lax.broadcasted_iota(i32, (n_lat, points), 0) == rel
    hits_f = hits.astype(f32)
    tri = (
        lax.broadcasted_iota(i32, (points, points), 0)
        < lax.broadcasted_iota(i32, (points, points), 1)
    ).astype(f32)
    before = jnp.dot(hits_f.astype(bf16), tri.astype(bf16), preferred_element_type=f32)
    slot = jnp.sum(before * hits_f, axis=0, keepdims=True).astype(i32)
    sid = rel * slots + slot
    limit = jnp.zeros((1, points), i32)
    for b in range(blocks):
        limit = jnp.where(lane // block_size == b, cnt_ref[b], limit)
    valid = (lane % block_size < limit).astype(i32)
    gath[0, 0:1, :] = sid
    gath[0, 1:2, :] = pos
    gath[0, 2:3, :] = valid
    gath[0, 3:4, :] = valid
    pl.semaphore_wait(barrier, n_lat - 1 + n_seg - 1)

    sends = {
        j: remote(gath.at[0], gath.at[j], gs_sem, gr_sem.at[j // group], (seg, lat_peers[j]))
        for j in far_first
    }
    for j in far_first:
        sends[j].start()
    sid_sends = [
        remote(gath.at[0], sid_in.at[m], ss_sem, sr_sem, (seg_peers[m], lat))
        for m in seg_far_first
    ]
    for copy in sid_sends:
        copy.start()

    pos_bits = 8
    bin_bits = (slice_bins - 1).bit_length()
    depth = min(256, slice_bins)
    depth_bits = depth.bit_length() - 1
    base = lat * (slice_bins << pos_bits)
    flag = slice_bins << pos_bits
    sub = lax.broadcasted_iota(i32, (slots, points), 0)
    bins = lax.broadcasted_iota(i32, (span, depth), 1)
    zero = jnp.zeros((span, depth), bf16)
    chunks = slice_bins // depth
    count = jnp.zeros((1, points), i32)
    col = jnp.zeros((1, width), f32)
    swap = quarter // 3

    def order(part_id):
        first, peers = part_id * group, lat_peers[part_id * group : (part_id + 1) * group]
        if part_id >= 2:
            other = 5 - part_id
            first = first + swap * (other - part_id) * group
            peers = [
                near + swap * (lat_peers[other * group + i] - near) for i, near in enumerate(peers)
            ]
        return first, peers

    def hand_on(src, j, g):
        for m in seg_far_first:
            copy = remote(
                src, far_rows.at[m, j], xs_sem, xr_sem.at[g], (seg_peers[m], lat)
            )
            copy.start()

    for part_id in range(PARTS):
        first, peers = order(part_id)
        rng = pl.ds(first, group) if part_id else pl.ds(1, group - 1)
        remote(gath.at[rng], gath.at[rng], gs_sem, gr_sem.at[first // group], (seg, peers[-1])).wait_recv()
        cols = []
        for i in range(group):
            j = first + i
            live_row = gath[j, 2:3, :]
            code = (gath[j, 1:2, :] - base + flag * (1 + live_row)).astype(f32)
            here = (gath[j, 0:1, :] - j * slots) == sub
            cols.append(jnp.sum(jnp.where(here, code, 0.0), axis=1, keepdims=True))
            count = count + live_row
        code = jnp.concatenate(cols, axis=0).astype(i32)
        kind = lax.shift_right_logical(code, bin_bits + pos_bits)
        low = lax.shift_right_logical(code & (flag - 1), pos_bits)
        upper = (code & ((1 << pos_bits) - 1)).astype(f32) * (1.0 / (1 << pos_bits))
        chunk = jnp.where(kind > 0, lax.shift_right_logical(low, depth_bits), -2)
        in_chunk = low & (depth - 1)
        local = jnp.where(bins == in_chunk, 1.0 - upper, 0.0)
        local = jnp.where(bins == ((in_chunk + 1) & (depth - 1)), upper, local).astype(bf16)
        where_id = jnp.where(bins < in_chunk, chunk + 1, chunk).astype(f32).astype(bf16)
        if part_id == 0:
            load.wait()
        weights = jnp.concatenate(
            [jnp.where(where_id == jnp.asarray(c, bf16), local, zero) for c in range(chunks)],
            axis=1,
        )
        held = jnp.dot(weights, coh[...], preferred_element_type=f32)
        for i in range(group):
            rows_out[first + i] = held[i * slots : (i + 1) * slots, :]
        col = col + jnp.sum(jnp.where(kind > 1, held, 0.0), axis=0, keepdims=True)
        for i in reversed(range(group)):
            if part_id == 0 and i == 0:
                continue
            j = first + i
            copy = remote(
                rows_out.at[j], rows_in.at[j], rs_sem, rr_sem.at[j], (seg, peers[i])
            )
            copy.start()
        if part_id == 0:
            hand_on(rows_out.at[0], 0, 0)
    col_out[0] = col
    for j in far_first:
        remote(col_out.at[0], col_in.at[j], cs_sem, cr_sem, (seg, lat_peers[j])).start()
    total_count = jnp.sum(count.astype(f32), axis=1, keepdims=True)

    for part_id in range(PARTS):
        first, peers = order(part_id)
        for i in range(group):
            j = first + i
            if part_id or i:
                remote(
                    rows_out.at[j], rows_in.at[j], rs_sem, rr_sem.at[j], (seg, peers[i])
                ).wait_recv()
                hand_on(rows_in.at[j], j, first // group)

    def tree(terms):
        w = 1
        while w < n_seg:
            terms = [terms[i] + terms[i + 1] for i in range(0, len(terms), 2)]
            w *= 2
        return terms[0]

    rng = pl.ds(1, n_lat - 1)
    seg_rng = pl.ds(1, n_seg - 1)
    cols = remote(col_in.at[rng], col_in.at[rng], cs_sem, cr_sem, (seg, lat_peers[1]))
    cols.wait_recv()
    for j in range(1, n_lat):
        col = col + col_in[j]
    psum[0] = col
    for m in seg_far_first:
        remote(psum.at[0], psum_in.at[m], ps_sem, pr_sem, (seg_peers[m], lat)).start()
    psums = remote(psum_in.at[seg_rng], psum_in.at[seg_rng], ps_sem, pr_sem, (seg_peers[1], lat))

    sids = remote(sid_in.at[seg_rng], sid_in.at[seg_rng], ss_sem, sr_sem, (seg_peers[1], lat))
    sids.wait_recv()
    slot_row = lax.broadcasted_iota(i32, (total_slots, points), 0)
    picks = []
    for m in range(n_seg):
        theirs = sid_in[m, 0:1, :] if m else sid
        picks.append((slot_row == theirs).astype(f32).T.astype(bf16))
    remote(gath.at[rng], gath.at[rng], gs_sem, gr_sem.at[0], (seg, lat_peers[1])).wait_send()
    remote(rows_out.at[rng], rows_in.at[rng], rs_sem, rr_sem.at[0], (seg, lat_peers[1])).wait_send()
    cols.wait_send()
    sids.wait_send()

    total = jnp.zeros((points, width), f32)
    for part_id in range(PARTS):
        first = part_id * group
        theirs = far_rows.at[seg_rng, pl.ds(first, group)]
        remote(theirs, theirs, xs_sem, xr_sem.at[part_id], (seg_peers[1], lat)).wait_recv()
        got = []
        mine = []
        for m in range(n_seg):
            mine.append(picks[m][:, first * slots : (first + group) * slots])
            for j in range(first, first + group):
                if m:
                    got.append(far_rows[m, j])
                else:
                    got.append(rows_in[j] if j else rows_out[0])
        got = jnp.concatenate(got, axis=0)
        high = got.astype(bf16)
        rest = (got - high.astype(f32)).astype(bf16)
        total = total + jnp.dot(
            jnp.concatenate(mine + mine, axis=1),
            jnp.concatenate([high, rest], axis=0),
            preferred_element_type=f32,
        )
    stat = total / n_seg
    semi_ref[...] = stat.astype(semi_ref.dtype)
    psums.wait_recv()
    col = tree([col] + [psum_in[m] for m in range(1, n_seg)])
    global_mean = (col / n_seg) / total_count
    row = lax.broadcasted_iota(i32, (block_size, width), 0)
    for b in range(blocks):
        block = stat[b * block_size : (b + 1) * block_size]
        block_sum = jnp.sum(jnp.where(row < cnt_ref[b], block, 0.0), axis=0, keepdims=True)
        mean = block_sum / jnp.full((1, width), cnt_ref[b], i32).astype(f32)
        excess_ref[b : b + 1, :] = mean - global_mean

    psums.wait_send()
    theirs = far_rows.at[seg_rng]
    remote(theirs, theirs, xs_sem, xr_sem.at[0], (seg_peers[1], lat)).wait_send()


def deliver(semi_ref, excess_ref, semi_out, excess_out, sem):
    copies = [
        pltpu.make_async_copy(semi_ref, semi_out, sem.at[0]),
        pltpu.make_async_copy(excess_ref, excess_out, sem.at[1]),
    ]
    for copy in copies:
        copy.start()
    for copy in copies:
        copy.wait()


def shards(n_lat, n_seg, coh_map, positions, counts):
    _, slice_bins, width = coh_map.shape
    points = positions.shape[1]
    blocks = counts.shape[0]
    slots = 2 * points // n_lat
    f32 = jnp.float32
    dma = pltpu.SemaphoreType.DMA
    made = pl.pallas_call(
        functools.partial(kernel, n_lat, n_seg),
        out_shape=(
            pltpu.VMEM((points, width), jnp.bfloat16),
            pltpu.VMEM((blocks, width), f32),
        ),
        in_specs=[
            pl.BlockSpec(memory_space=pl.ANY),
            pl.BlockSpec(memory_space=pl.ANY),
            pl.BlockSpec(memory_space=pl.ANY),
        ],
        out_specs=(
            pl.BlockSpec(memory_space=pltpu.VMEM),
            pl.BlockSpec(memory_space=pltpu.VMEM),
        ),
        scratch_shapes=[
            pltpu.VMEM((1, points), jnp.int32),
            pltpu.SMEM((blocks,), jnp.int32),
            pltpu.VMEM((slice_bins, width), coh_map.dtype),
            pltpu.VMEM((n_lat, 4, points), jnp.int32),
            pltpu.VMEM((n_lat, slots, width), f32),
            pltpu.VMEM((n_lat, slots, width), f32),
            pltpu.VMEM((1, 1, width), f32),
            pltpu.VMEM((n_lat, 1, width), f32),
            pltpu.VMEM((n_seg, 4, points), jnp.int32),
            pltpu.VMEM((n_seg, n_lat, slots, width), f32),
            pltpu.VMEM((1, 1, width), f32),
            pltpu.VMEM((n_seg, 1, width), f32),
            dma,
            dma,
            dma((PARTS,)),
            dma,
            dma((n_lat,)),
            dma,
            dma,
            dma,
            dma((PARTS,)),
            dma,
            dma,
            dma,
            dma,
            dma((2,)),
        ],
        compiler_params=pltpu.CompilerParams(collective_id=0, has_side_effects=True),
    )(positions, counts, coh_map)
    made = [pltpu.with_memory_space_constraint(x, pltpu.VMEM) for x in made]
    return pl.pallas_call(
        deliver,
        out_shape=tuple(jax.ShapeDtypeStruct(x.shape, x.dtype) for x in made),
        in_specs=[pl.BlockSpec(memory_space=pltpu.VMEM)] * 2,
        out_specs=(pl.BlockSpec(memory_space=pl.ANY),) * 2,
        scratch_shapes=[dma((2,))],
    )(*made)


def solution(mesh):
    in_specs = (P("seg", "lat", None), P("seg", "lat"), P("lat"))
    out_specs = (P("lat", None), P("lat", None))
    body = functools.partial(shards, mesh.shape["lat"], mesh.shape["seg"])
    return jax.shard_map(body, mesh=mesh, in_specs=in_specs, out_specs=out_specs, check_vma=False)
```

time: 21.7 us -> 21.1 us (0.972)
  Pallas kernels: 20.9 us -> 20.3 us
    pallas_call x1, Pallas kernels: 20.3 us -> 19.7 us  [shards(): pl.pallas_call(functools.partial(kernel, n_lat, n_seg), out_shape=(pltpu....]
where the time goes in v1:
time: 21.1 us; the launch traced here: 21 us
  Pallas kernels  20.3 us (96%)
  between operations  0.64 us (3%)
    pallas_call x1, Pallas kernels, shards(): pl.pallas_call(functools.partial(kernel, n_lat, n_seg), out_shape=(pltpu....  19.7 us
    pallas_call x1, Pallas kernels, shards(): pl.pallas_call(deliver, out_shape=tuple((jax.ShapeDtypeStruct(x.shape, x....  0.64 us

profile of v1, /device:TPU:0, one launch (start us, length us, event | category | flops | bytes accessed | tf_op | source)
XLA Modules:
  0.0 21.0 jit_solution(8058103801175612875)
XLA Ops:
  0.6 19.7 %shard_map.50 = (bf16[128,128]{1,0:T(8,128)(2,1)S(1)}, f32[2,128]{1,0:T(2,128)S(1)}) custom-call(s32[1,128]{1,0:T(1,128)} %pos_hbm.1, s32[2]{0:T(128)} %cnt_hbm.1, bf16[1,8192,128]{2,1,0:T(8,128)(2,1)} %coh_hbm.1), custom_call_target="tpu_custom_call" | custom-call | tf_op jit(solution)/shard_map/pallas_call | solution.py:313
  20.3 0.6 %shard_map.51 = (bf16[128,128]{1,0:T(8,128)(2,1)}, f32[2,128]{1,0:T(2,128)}) custom-call(bf16[128,128]{1,0:T(8,128)(2,1)S(1)} %get-tuple-element.4.semi_ref, f32[2,128]{1,0:T(2,128)S(1)} %get-tuple-element.5.excess_ref), custom_call_target="tpu_custom_call" | custom-call | tf_op jit(solution)/shard_map/pallas_call | solution.py:359

commit v2 on v1

--- a/solution.py
+++ b/solution.py
@@ -9,6 +9,8 @@
 
 MESH = pl.DeviceIdType.MESH
 PARTS = 4
+STEPS = (((0, 0, 0, 0),), ((1, 1, 2, 1),), ((2, 3, 1, 3), (3, 2, 3, 2)))
+ARRIVE = ((0, 0, 0, 0), (1, 1, 1, 1), (2, 3, 3, 2), (3, 2, 2, 3))
 
 
 def flip(index, mask):
@@ -66,7 +68,6 @@
     total_slots = n_lat * slots
     f32, bf16, i32 = jnp.float32, jnp.bfloat16, jnp.int32
     group = n_lat // PARTS
-    span = group * slots
     quarter = lat // group
 
     def remote(src, dst, send_sem, recv_sem, to):
@@ -143,21 +144,24 @@
     base = lat * (slice_bins << pos_bits)
     flag = slice_bins << pos_bits
     sub = lax.broadcasted_iota(i32, (slots, points), 0)
-    bins = lax.broadcasted_iota(i32, (span, depth), 1)
-    zero = jnp.zeros((span, depth), bf16)
     chunks = slice_bins // depth
     count = jnp.zeros((1, points), i32)
     col = jnp.zeros((1, width), f32)
-    swap = quarter // 3
-
-    def order(part_id):
-        first, peers = part_id * group, lat_peers[part_id * group : (part_id + 1) * group]
-        if part_id >= 2:
-            other = 5 - part_id
-            first = first + swap * (other - part_id) * group
-            peers = [
-                near + swap * (lat_peers[other * group + i] - near) for i, near in enumerate(peers)
-            ]
+    late = quarter // 3
+    third = quarter // 2 - late
+    second = quarter - 2 * third - 3 * late
+
+    def mixed(plain, in_second, in_third, in_last):
+        return (
+            plain
+            + second * (in_second - plain)
+            + third * (in_third - plain)
+            + late * (in_last - plain)
+        )
+
+    def order(turns):
+        first = mixed(*turns) * group
+        peers = [mixed(*(lat_peers[g * group + i] for g in turns)) for i in range(group)]
         return first, peers
 
     def hand_on(src, j, g):
@@ -167,57 +171,69 @@
             )
             copy.start()
 
-    for part_id in range(PARTS):
-        first, peers = order(part_id)
-        rng = pl.ds(first, group) if part_id else pl.ds(1, group - 1)
-        remote(gath.at[rng], gath.at[rng], gs_sem, gr_sem.at[first // group], (seg, peers[-1])).wait_recv()
+    parity = lax.rem(lat, 2)
+    for step, turns in enumerate(STEPS):
+        places = [order(t) if step else (0, lat_peers[:group]) for t in turns]
         cols = []
-        for i in range(group):
-            j = first + i
-            live_row = gath[j, 2:3, :]
-            code = (gath[j, 1:2, :] - base + flag * (1 + live_row)).astype(f32)
-            here = (gath[j, 0:1, :] - j * slots) == sub
-            cols.append(jnp.sum(jnp.where(here, code, 0.0), axis=1, keepdims=True))
-            count = count + live_row
+        for first, peers in places:
+            rng = pl.ds(first, group) if step else pl.ds(1, group - 1)
+            remote(
+                gath.at[rng], gath.at[rng], gs_sem, gr_sem.at[first // group], (seg, peers[-1])
+            ).wait_recv()
+            for i in range(group):
+                j = first + i
+                live_row = gath[j, 2:3, :]
+                code = (gath[j, 1:2, :] - base + flag * (1 + live_row)).astype(f32)
+                here = (gath[j, 0:1, :] - j * slots) == sub
+                cols.append(jnp.sum(jnp.where(here, code, 0.0), axis=1, keepdims=True))
+                count = count + live_row
         code = jnp.concatenate(cols, axis=0).astype(i32)
         kind = lax.shift_right_logical(code, bin_bits + pos_bits)
         low = lax.shift_right_logical(code & (flag - 1), pos_bits)
         upper = (code & ((1 << pos_bits) - 1)).astype(f32) * (1.0 / (1 << pos_bits))
         chunk = jnp.where(kind > 0, lax.shift_right_logical(low, depth_bits), -2)
         in_chunk = low & (depth - 1)
+        bins = lax.broadcasted_iota(i32, (code.shape[0], depth), 1)
+        zero = jnp.zeros(bins.shape, bf16)
         local = jnp.where(bins == in_chunk, 1.0 - upper, 0.0)
         local = jnp.where(bins == ((in_chunk + 1) & (depth - 1)), upper, local).astype(bf16)
         where_id = jnp.where(bins < in_chunk, chunk + 1, chunk).astype(f32).astype(bf16)
-        if part_id == 0:
+        if step == 0:
             load.wait()
         weights = jnp.concatenate(
             [jnp.where(where_id == jnp.asarray(c, bf16), local, zero) for c in range(chunks)],
             axis=1,
         )
         held = jnp.dot(weights, coh[...], preferred_element_type=f32)
-        for i in range(group):
-            rows_out[first + i] = held[i * slots : (i + 1) * slots, :]
+        for n, (first, peers) in enumerate(places):
+            for i in range(group):
+                at = (n * group + i) * slots
+                rows_out[first + i] = held[at : at + slots, :]
+            if step == 0:
+                for j in range(1, group):
+                    remote(
+                        rows_out.at[j], rows_in.at[j], rs_sem, rr_sem.at[j], (seg, lat_peers[j])
+                    ).start()
+                hand_on(rows_out.at[0], 0, 0)
+                continue
+            for i in range(group):
+                turn = parity if i % 2 == 0 else -parity
+                j = first + i + turn
+                peer = peers[i] + parity * (peers[i ^ 1] - peers[i])
+                remote(
+                    rows_out.at[j], rows_in.at[j], rs_sem, rr_sem.at[j], (seg, peer)
+                ).start()
         col = col + jnp.sum(jnp.where(kind > 1, held, 0.0), axis=0, keepdims=True)
-        for i in reversed(range(group)):
-            if part_id == 0 and i == 0:
-                continue
-            j = first + i
-            copy = remote(
-                rows_out.at[j], rows_in.at[j], rs_sem, rr_sem.at[j], (seg, peers[i])
-            )
-            copy.start()
-        if part_id == 0:
-            hand_on(rows_out.at[0], 0, 0)
     col_out[0] = col
-    for j in far_first:
-        remote(col_out.at[0], col_in.at[j], cs_sem, cr_sem, (seg, lat_peers[j])).start()
+    for m in seg_far_first:
+        remote(col_out.at[0], psum_in.at[m], ps_sem, pr_sem, (seg_peers[m], lat)).start()
     total_count = jnp.sum(count.astype(f32), axis=1, keepdims=True)
 
-    for part_id in range(PARTS):
-        first, peers = order(part_id)
+    for g, turns in enumerate(ARRIVE):
+        first, peers = order(turns) if g else (0, lat_peers[:group])
         for i in range(group):
             j = first + i
-            if part_id or i:
+            if g or i:
                 remote(
                     rows_out.at[j], rows_in.at[j], rs_sem, rr_sem.at[j], (seg, peers[i])
                 ).wait_recv()
@@ -232,14 +248,13 @@
 
     rng = pl.ds(1, n_lat - 1)
     seg_rng = pl.ds(1, n_seg - 1)
+    psums = remote(psum_in.at[seg_rng], psum_in.at[seg_rng], ps_sem, pr_sem, (seg_peers[1], lat))
+    psums.wait_recv()
+    col = tree([col] + [psum_in[m] for m in range(1, n_seg)])
+    psum[0] = col
+    for j in far_first:
+        remote(psum.at[0], col_in.at[j], cs_sem, cr_sem, (seg, lat_peers[j])).start()
     cols = remote(col_in.at[rng], col_in.at[rng], cs_sem, cr_sem, (seg, lat_peers[1]))
-    cols.wait_recv()
-    for j in range(1, n_lat):
-        col = col + col_in[j]
-    psum[0] = col
-    for m in seg_far_first:
-        remote(psum.at[0], psum_in.at[m], ps_sem, pr_sem, (seg_peers[m], lat)).start()
-    psums = remote(psum_in.at[seg_rng], psum_in.at[seg_rng], ps_sem, pr_sem, (seg_peers[1], lat))
 
     sids = remote(sid_in.at[seg_rng], sid_in.at[seg_rng], ss_sem, sr_sem, (seg_peers[1], lat))
     sids.wait_recv()
@@ -250,7 +265,7 @@
         picks.append((slot_row == theirs).astype(f32).T.astype(bf16))
     remote(gath.at[rng], gath.at[rng], gs_sem, gr_sem.at[0], (seg, lat_peers[1])).wait_send()
     remote(rows_out.at[rng], rows_in.at[rng], rs_sem, rr_sem.at[0], (seg, lat_peers[1])).wait_send()
-    cols.wait_send()
+    psums.wait_send()
     sids.wait_send()
 
     total = jnp.zeros((points, width), f32)
@@ -277,8 +292,9 @@
         )
     stat = total / n_seg
     semi_ref[...] = stat.astype(semi_ref.dtype)
-    psums.wait_recv()
-    col = tree([col] + [psum_in[m] for m in range(1, n_seg)])
+    cols.wait_recv()
+    for j in range(1, n_lat):
+        col = col + col_in[j]
     global_mean = (col / n_seg) / total_count
     row = lax.broadcasted_iota(i32, (block_size, width), 0)
     for b in range(blocks):
@@ -287,7 +303,7 @@
         mean = block_sum / jnp.full((1, width), cnt_ref[b], i32).astype(f32)
         excess_ref[b : b + 1, :] = mean - global_mean
 
-    psums.wait_send()
+    cols.wait_send()
     theirs = far_rows.at[seg_rng]
     remote(theirs, theirs, xs_sem, xr_sem.at[0], (seg_peers[1], lat)).wait_send()
 

time: 21.1 us -> 20.4 us (0.967)
  Pallas kernels: 20.3 us -> 19.6 us
    pallas_call x1, Pallas kernels: 19.7 us -> 19 us  [shards(): pl.pallas_call(functools.partial(kernel, n_lat, n_seg), out_shape=(pltpu....]
where the time goes in v2:
time: 20.4 us; the launch traced here: 20.2 us
  Pallas kernels  19.6 us (96%)
  between operations  0.64 us (3%)
    pallas_call x1, Pallas kernels, shards(): pl.pallas_call(functools.partial(kernel, n_lat, n_seg), out_shape=(pltpu....  19 us
    pallas_call x1, Pallas kernels, shards(): pl.pallas_call(deliver, out_shape=tuple((jax.ShapeDtypeStruct(x.shape, x....  0.64 us

profile of v2, /device:TPU:0, one launch (start us, length us, event | category | flops | bytes accessed | tf_op | source)
XLA Modules:
  0.0 20.2 jit_solution(6997104619657933140)
XLA Ops:
  0.6 19.0 %shard_map.50 = (bf16[128,128]{1,0:T(8,128)(2,1)S(1)}, f32[2,128]{1,0:T(2,128)S(1)}) custom-call(s32[1,128]{1,0:T(1,128)} %pos_hbm.1, s32[2]{0:T(128)} %cnt_hbm.1, bf16[1,8192,128]{2,1,0:T(8,128)(2,1)} %coh_hbm.1), custom_call_target="tpu_custom_call" | custom-call | tf_op jit(solution)/shard_map/pallas_call | solution.py:329
  19.6 0.6 %shard_map.51 = (bf16[128,128]{1,0:T(8,128)(2,1)}, f32[2,128]{1,0:T(2,128)}) custom-call(bf16[128,128]{1,0:T(8,128)(2,1)S(1)} %get-tuple-element.4.semi_ref, f32[2,128]{1,0:T(2,128)S(1)} %get-tuple-element.5.excess_ref), custom_call_target="tpu_custom_call" | custom-call | tf_op jit(solution)/shard_map/pallas_call | solution.py:375

commit v3 on v2

--- a/solution.py
+++ b/solution.py
@@ -9,6 +9,7 @@
 
 MESH = pl.DeviceIdType.MESH
 PARTS = 4
+DIRECT = ((0, 1), (0, 3), (1, 2))
 STEPS = (((0, 0, 0, 0),), ((1, 1, 2, 1),), ((2, 3, 1, 3), (3, 2, 3, 2)))
 ARRIVE = ((0, 0, 0, 0), (1, 1, 1, 1), (2, 3, 3, 2), (3, 2, 2, 3))
 
@@ -57,6 +58,7 @@
     ps_sem,
     pr_sem,
     in_sem,
+    ds_sem,
 ):
     lat = lax.axis_index("lat")
     seg = lax.axis_index("seg")
@@ -69,6 +71,11 @@
     f32, bf16, i32 = jnp.float32, jnp.bfloat16, jnp.int32
     group = n_lat // PARTS
     quarter = lat // group
+    parity = lax.rem(lat, 2)
+    late = quarter // 3
+    third = quarter // 2 - late
+    second = quarter - 2 * third - 3 * late
+    is_quarter = (1 - second - third - late, second, third, late)
 
     def remote(src, dst, send_sem, recv_sem, to):
         return pltpu.make_async_remote_copy(
@@ -89,6 +96,15 @@
         pl.semaphore_signal(barrier, inc=1, device_id=(seg, lat_peers[j]), device_id_type=MESH)
     for m in seg_far_first:
         pl.semaphore_signal(barrier, inc=1, device_id=(seg_peers[m], lat), device_id_type=MESH)
+
+    for owner, g in DIRECT:
+
+        @pl.when((quarter == owner) & (parity == 0))
+        def _(g=g):
+            for j in range(g * group, (g + 1) * group):
+                pl.semaphore_signal(
+                    barrier, inc=1, device_id=(seg_peers[-1], lat_peers[j]), device_id_type=MESH
+                )
 
     small = [
         pltpu.make_async_copy(pos_hbm, pos_ref, in_sem.at[0]),
@@ -122,7 +138,9 @@
     gath[0, 1:2, :] = pos
     gath[0, 2:3, :] = valid
     gath[0, 3:4, :] = valid
-    pl.semaphore_wait(barrier, n_lat - 1 + n_seg - 1)
+
+    straight = sum(is_quarter[owner ^ g] for owner, g in DIRECT)
+    pl.semaphore_wait(barrier, n_lat - 1 + n_seg - 1 + straight * (group // 2))
 
     sends = {
         j: remote(gath.at[0], gath.at[j], gs_sem, gr_sem.at[j // group], (seg, lat_peers[j]))
@@ -147,10 +165,6 @@
     chunks = slice_bins // depth
     count = jnp.zeros((1, points), i32)
     col = jnp.zeros((1, width), f32)
-    late = quarter // 3
-    third = quarter // 2 - late
-    second = quarter - 2 * third - 3 * late
-
     def mixed(plain, in_second, in_third, in_last):
         return (
             plain
@@ -164,14 +178,18 @@
         peers = [mixed(*(lat_peers[g * group + i] for g in turns)) for i in range(group)]
         return first, peers
 
-    def hand_on(src, j, g):
+    def hand_on(src, j, g, turn=0):
         for m in seg_far_first:
             copy = remote(
-                src, far_rows.at[m, j], xs_sem, xr_sem.at[g], (seg_peers[m], lat)
+                src, far_rows.at[m * n_lat + j], xs_sem, xr_sem.at[g], (seg_peers[m], lat)
             )
-            copy.start()
-
-    parity = lax.rem(lat, 2)
+            skips = [owner for owner, r in DIRECT if ARRIVE[turn][owner] == r]
+            if turn and skips and m == n_seg - 1:
+                skip = sum(is_quarter[owner] for owner in skips) * (1 - parity)
+                pl.when(skip == 0)(copy.start)
+            else:
+                copy.start()
+
     for step, turns in enumerate(STEPS):
         places = [order(t) if step else (0, lat_peers[:group]) for t in turns]
         cols = []
@@ -205,6 +223,7 @@
             axis=1,
         )
         held = jnp.dot(weights, coh[...], preferred_element_type=f32)
+        posts, crosses = [], []
         for n, (first, peers) in enumerate(places):
             for i in range(group):
                 at = (n * group + i) * slots
@@ -216,28 +235,41 @@
                     ).start()
                 hand_on(rows_out.at[0], 0, 0)
                 continue
-            for i in range(group):
-                turn = parity if i % 2 == 0 else -parity
-                j = first + i + turn
-                peer = peers[i] + parity * (peers[i ^ 1] - peers[i])
-                remote(
-                    rows_out.at[j], rows_in.at[j], rs_sem, rr_sem.at[j], (seg, peer)
-                ).start()
+            def post(odd, first=first, peers=peers):
+                for i in range(odd, group, 2):
+                    turn = parity if odd == 0 else -parity
+                    j = first + i + turn
+                    peer = peers[i] + parity * (peers[i ^ 1] - peers[i])
+                    remote(
+                        rows_out.at[j], rows_in.at[j], rs_sem, rr_sem.at[j], (seg, peer)
+                    ).start()
+
+            def across(first=first, peers=peers):
+                for i in range(0, group, 2):
+                    j = first + i + parity
+                    peer = peers[i] + parity * (peers[i + 1] - peers[i])
+                    remote(
+                        rows_out.at[j],
+                        far_rows.at[(n_seg - 1) * n_lat + j],
+                        ds_sem,
+                        xr_sem.at[first // group],
+                        (seg_peers[-1], peer),
+                    ).start()
+
+            posts.append(post)
+            crosses.append(across)
+        for what, n in ((0, 0), (1, 0), (2, 0), (0, 1), (1, 1), (2, 1)) if step == 2 else ((0, 0), (1, 0), (2, 0)) if step else ():
+            if what < 2:
+                posts[n](what)
+                continue
+            makers = [owner ^ r for owner, r in DIRECT if turns[n][owner ^ r] == r]
+            if makers:
+                pl.when(sum(is_quarter[q] for q in makers) == 1)(crosses[n])
         col = col + jnp.sum(jnp.where(kind > 1, held, 0.0), axis=0, keepdims=True)
     col_out[0] = col
     for m in seg_far_first:
         remote(col_out.at[0], psum_in.at[m], ps_sem, pr_sem, (seg_peers[m], lat)).start()
     total_count = jnp.sum(count.astype(f32), axis=1, keepdims=True)
-
-    for g, turns in enumerate(ARRIVE):
-        first, peers = order(turns) if g else (0, lat_peers[:group])
-        for i in range(group):
-            j = first + i
-            if g or i:
-                remote(
-                    rows_out.at[j], rows_in.at[j], rs_sem, rr_sem.at[j], (seg, peers[i])
-                ).wait_recv()
-                hand_on(rows_in.at[j], j, first // group)
 
     def tree(terms):
         w = 1
@@ -249,12 +281,22 @@
     rng = pl.ds(1, n_lat - 1)
     seg_rng = pl.ds(1, n_seg - 1)
     psums = remote(psum_in.at[seg_rng], psum_in.at[seg_rng], ps_sem, pr_sem, (seg_peers[1], lat))
-    psums.wait_recv()
-    col = tree([col] + [psum_in[m] for m in range(1, n_seg)])
-    psum[0] = col
-    for j in far_first:
-        remote(psum.at[0], col_in.at[j], cs_sem, cr_sem, (seg, lat_peers[j])).start()
     cols = remote(col_in.at[rng], col_in.at[rng], cs_sem, cr_sem, (seg, lat_peers[1]))
+    for turn, turns in enumerate(ARRIVE):
+        if turn == 2:
+            psums.wait_recv()
+            col = tree([col] + [psum_in[m] for m in range(1, n_seg)])
+            psum[0] = col
+            for j in far_first:
+                remote(psum.at[0], col_in.at[j], cs_sem, cr_sem, (seg, lat_peers[j])).start()
+        first, peers = order(turns) if turn else (0, lat_peers[:group])
+        for i in range(group):
+            j = first + i
+            if turn or i:
+                remote(
+                    rows_out.at[j], rows_in.at[j], rs_sem, rr_sem.at[j], (seg, peers[i])
+                ).wait_recv()
+                hand_on(rows_in.at[j], j, first // group, turn)
 
     sids = remote(sid_in.at[seg_rng], sid_in.at[seg_rng], ss_sem, sr_sem, (seg_peers[1], lat))
     sids.wait_recv()
@@ -271,7 +313,7 @@
     total = jnp.zeros((points, width), f32)
     for part_id in range(PARTS):
         first = part_id * group
-        theirs = far_rows.at[seg_rng, pl.ds(first, group)]
+        theirs = far_rows.at[pl.ds(0, (n_seg - 1) * group)]
         remote(theirs, theirs, xs_sem, xr_sem.at[part_id], (seg_peers[1], lat)).wait_recv()
         got = []
         mine = []
@@ -279,7 +321,7 @@
             mine.append(picks[m][:, first * slots : (first + group) * slots])
             for j in range(first, first + group):
                 if m:
-                    got.append(far_rows[m, j])
+                    got.append(far_rows[m * n_lat + j])
                 else:
                     got.append(rows_in[j] if j else rows_out[0])
         got = jnp.concatenate(got, axis=0)
@@ -304,8 +346,21 @@
         excess_ref[b : b + 1, :] = mean - global_mean
 
     cols.wait_send()
-    theirs = far_rows.at[seg_rng]
-    remote(theirs, theirs, xs_sem, xr_sem.at[0], (seg_peers[1], lat)).wait_send()
+
+    def sent(blocks, sem):
+        ref = far_rows.at[pl.ds(0, blocks)]
+        remote(ref, ref, sem, xr_sem.at[0], (seg_peers[1], lat)).wait_send()
+
+    for q in range(PARTS):
+        skipped = group * sum(owner == q for owner, _ in DIRECT)
+        across = group // 2 * sum(owner ^ g == q for owner, g in DIRECT)
+        for core in range(2):
+
+            @pl.when((quarter == q) & (parity == core))
+            def _(skipped=skipped, across=across, core=core):
+                sent((n_seg - 1) * n_lat - (0 if core else skipped), xs_sem)
+                if across:
+                    sent(across, ds_sem)
 
 
 def deliver(semi_ref, excess_ref, semi_out, excess_out, sem):
@@ -351,7 +406,7 @@
             pltpu.VMEM((1, 1, width), f32),
             pltpu.VMEM((n_lat, 1, width), f32),
             pltpu.VMEM((n_seg, 4, points), jnp.int32),
-            pltpu.VMEM((n_seg, n_lat, slots, width), f32),
+            pltpu.VMEM((n_seg * n_lat, slots, width), f32),
             pltpu.VMEM((1, 1, width), f32),
             pltpu.VMEM((n_seg, 1, width), f32),
             dma,
@@ -368,6 +423,7 @@
             dma,
             dma,
             dma((2,)),
+            dma,
         ],
         compiler_params=pltpu.CompilerParams(collective_id=0, has_side_effects=True),
     )(positions, counts, coh_map)

time: 20.4 us -> 19.7 us (0.966)
  the two profiles are of different devices: /device:TPU:0 before, /device:TPU:9 now
where the time goes in v3:
time: 19.7 us; the launch traced here: 19.6 us
  Pallas kernels  18.9 us (96%)
  between operations  0.64 us (3%)
    pallas_call x1, Pallas kernels, shards(): pl.pallas_call(functools.partial(kernel, n_lat, n_seg), out_shape=(pltpu....  18.3 us
    pallas_call x1, Pallas kernels, shards(): pl.pallas_call(deliver, out_shape=tuple((jax.ShapeDtypeStruct(x.shape, x....  0.64 us

profile of v3, /device:TPU:9, one launch (start us, length us, event | category | flops | bytes accessed | tf_op | source)
XLA Modules:
  0.0 19.6 jit_solution(13046836993720805790)
XLA Ops:
  0.6 18.3 %shard_map.50 = (bf16[128,128]{1,0:T(8,128)(2,1)S(1)}, f32[2,128]{1,0:T(2,128)S(1)}) custom-call(s32[1,128]{1,0:T(1,128)} %pos_hbm.1, s32[2]{0:T(128)} %cnt_hbm.1, bf16[1,8192,128]{2,1,0:T(8,128)(2,1)} %coh_hbm.1), custom_call_target="tpu_custom_call" | custom-call | tf_op jit(solution)/shard_map/pallas_call | solution.py:384
  18.9 0.6 %shard_map.51 = (bf16[128,128]{1,0:T(8,128)(2,1)}, f32[2,128]{1,0:T(2,128)}) custom-call(bf16[128,128]{1,0:T(8,128)(2,1)S(1)} %get-tuple-element.4.semi_ref, f32[2,128]{1,0:T(2,128)S(1)} %get-tuple-element.5.excess_ref), custom_call_target="tpu_custom_call" | custom-call | tf_op jit(solution)/shard_map/pallas_call | solution.py:431

commit v4 on v3

--- a/solution.py
+++ b/solution.py
@@ -40,10 +40,8 @@
     rows_in,
     col_out,
     col_in,
-    sid_in,
     far_rows,
     psum,
-    psum_in,
     coh_sem,
     gs_sem,
     gr_sem,
@@ -51,14 +49,10 @@
     rr_sem,
     cs_sem,
     cr_sem,
-    xs_sem,
     xr_sem,
-    ss_sem,
     sr_sem,
-    ps_sem,
     pr_sem,
     in_sem,
-    ds_sem,
 ):
     lat = lax.axis_index("lat")
     seg = lax.axis_index("seg")
@@ -149,7 +143,7 @@
     for j in far_first:
         sends[j].start()
     sid_sends = [
-        remote(gath.at[0], sid_in.at[m], ss_sem, sr_sem, (seg_peers[m], lat))
+        remote(gath.at[0], gath.at[n_lat + m], gs_sem, sr_sem, (seg_peers[m], lat))
         for m in seg_far_first
     ]
     for copy in sid_sends:
@@ -165,6 +159,7 @@
     chunks = slice_bins // depth
     count = jnp.zeros((1, points), i32)
     col = jnp.zeros((1, width), f32)
+
     def mixed(plain, in_second, in_third, in_last):
         return (
             plain
@@ -181,7 +176,7 @@
     def hand_on(src, j, g, turn=0):
         for m in seg_far_first:
             copy = remote(
-                src, far_rows.at[m * n_lat + j], xs_sem, xr_sem.at[g], (seg_peers[m], lat)
+                src, far_rows.at[m * n_lat + j], rs_sem, xr_sem.at[g - (g + PARTS - 1) // PARTS], (seg_peers[m], lat)
             )
             skips = [owner for owner, r in DIRECT if ARRIVE[turn][owner] == r]
             if turn and skips and m == n_seg - 1:
@@ -231,7 +226,7 @@
             if step == 0:
                 for j in range(1, group):
                     remote(
-                        rows_out.at[j], rows_in.at[j], rs_sem, rr_sem.at[j], (seg, lat_peers[j])
+                        rows_out.at[j], rows_in.at[j], rs_sem, rr_sem.at[j - 1], (seg, lat_peers[j])
                     ).start()
                 hand_on(rows_out.at[0], 0, 0)
                 continue
@@ -241,7 +236,7 @@
                     j = first + i + turn
                     peer = peers[i] + parity * (peers[i ^ 1] - peers[i])
                     remote(
-                        rows_out.at[j], rows_in.at[j], rs_sem, rr_sem.at[j], (seg, peer)
+                        rows_out.at[j], rows_in.at[j], rs_sem, rr_sem.at[j - 1], (seg, peer)
                     ).start()
 
             def across(first=first, peers=peers):
@@ -251,14 +246,14 @@
                     remote(
                         rows_out.at[j],
                         far_rows.at[(n_seg - 1) * n_lat + j],
-                        ds_sem,
-                        xr_sem.at[first // group],
+                        rs_sem,
+                        xr_sem.at[first // group - 1],
                         (seg_peers[-1], peer),
                     ).start()
 
             posts.append(post)
             crosses.append(across)
-        for what, n in ((0, 0), (1, 0), (2, 0), (0, 1), (1, 1), (2, 1)) if step == 2 else ((0, 0), (1, 0), (2, 0)) if step else ():
+        for what, n in ((0, 0), (1, 0), (1, 1), (2, 0), (0, 1), (2, 1)) if step == 2 else ((0, 0), (1, 0), (2, 0)) if step else ():
             if what < 2:
                 posts[n](what)
                 continue
@@ -268,7 +263,7 @@
         col = col + jnp.sum(jnp.where(kind > 1, held, 0.0), axis=0, keepdims=True)
     col_out[0] = col
     for m in seg_far_first:
-        remote(col_out.at[0], psum_in.at[m], ps_sem, pr_sem, (seg_peers[m], lat)).start()
+        remote(col_out.at[0], col_in.at[n_lat + m], cs_sem, pr_sem, (seg_peers[m], lat)).start()
     total_count = jnp.sum(count.astype(f32), axis=1, keepdims=True)
 
     def tree(terms):
@@ -278,48 +273,52 @@
             w *= 2
         return terms[0]
 
-    rng = pl.ds(1, n_lat - 1)
-    seg_rng = pl.ds(1, n_seg - 1)
-    psums = remote(psum_in.at[seg_rng], psum_in.at[seg_rng], ps_sem, pr_sem, (seg_peers[1], lat))
-    cols = remote(col_in.at[rng], col_in.at[rng], cs_sem, cr_sem, (seg, lat_peers[1]))
+    lat_cols, seg_cols = col_in.at[pl.ds(1, n_lat - 1)], col_in.at[pl.ds(n_lat + 1, n_seg - 1)]
+
+    def seg_sum():
+        remote(seg_cols, seg_cols, cs_sem, pr_sem, (seg_peers[1], lat)).wait_recv()
+        psum[0] = tree([col_out[0]] + [col_in[n_lat + m] for m in range(1, n_seg)])
+        for j in far_first:
+            remote(psum.at[0], col_in.at[j], cs_sem, cr_sem, (seg, lat_peers[j])).start()
+
     for turn, turns in enumerate(ARRIVE):
         if turn == 2:
-            psums.wait_recv()
-            col = tree([col] + [psum_in[m] for m in range(1, n_seg)])
-            psum[0] = col
-            for j in far_first:
-                remote(psum.at[0], col_in.at[j], cs_sem, cr_sem, (seg, lat_peers[j])).start()
+            pl.when(quarter >= 2)(seg_sum)
+        elif turn == 3:
+            pl.when(jnp.logical_not(quarter >= 2))(seg_sum)
         first, peers = order(turns) if turn else (0, lat_peers[:group])
         for i in range(group):
             j = first + i
             if turn or i:
                 remote(
-                    rows_out.at[j], rows_in.at[j], rs_sem, rr_sem.at[j], (seg, peers[i])
+                    rows_out.at[j], rows_in.at[j], rs_sem, rr_sem.at[j - 1], (seg, peers[i])
                 ).wait_recv()
                 hand_on(rows_in.at[j], j, first // group, turn)
 
-    sids = remote(sid_in.at[seg_rng], sid_in.at[seg_rng], ss_sem, sr_sem, (seg_peers[1], lat))
-    sids.wait_recv()
+    theirs = gath.at[pl.ds(n_lat + 1, n_seg - 1)]
+    remote(theirs, theirs, gs_sem, sr_sem, (seg_peers[1], lat)).wait_recv()
     slot_row = lax.broadcasted_iota(i32, (total_slots, points), 0)
     picks = []
     for m in range(n_seg):
-        theirs = sid_in[m, 0:1, :] if m else sid
+        theirs = gath[n_lat + m, 0:1, :] if m else sid
         picks.append((slot_row == theirs).astype(f32).T.astype(bf16))
-    remote(gath.at[rng], gath.at[rng], gs_sem, gr_sem.at[0], (seg, lat_peers[1])).wait_send()
-    remote(rows_out.at[rng], rows_in.at[rng], rs_sem, rr_sem.at[0], (seg, lat_peers[1])).wait_send()
-    psums.wait_send()
-    sids.wait_send()
+    peers = n_lat - 1 + n_seg - 1
+
+    def sent(ref, sem):
+        remote(ref, ref, sem, sr_sem, (seg_peers[1], lat)).wait_send()
+
+    sent(gath.at[pl.ds(0, peers)], gs_sem)
 
     total = jnp.zeros((points, width), f32)
-    for part_id in range(PARTS):
-        first = part_id * group
-        theirs = far_rows.at[pl.ds(0, (n_seg - 1) * group)]
-        remote(theirs, theirs, xs_sem, xr_sem.at[part_id], (seg_peers[1], lat)).wait_recv()
+    for part_id in range(PARTS - 1):
+        first, last = (part_id + 1 if part_id else 0) * group, (part_id + 2) * group
+        theirs = far_rows.at[pl.ds(0, (n_seg - 1) * (last - first))]
+        remote(theirs, theirs, rs_sem, xr_sem.at[part_id], (seg_peers[1], lat)).wait_recv()
         got = []
         mine = []
         for m in range(n_seg):
-            mine.append(picks[m][:, first * slots : (first + group) * slots])
-            for j in range(first, first + group):
+            mine.append(picks[m][:, first * slots : last * slots])
+            for j in range(first, last):
                 if m:
                     got.append(far_rows[m * n_lat + j])
                 else:
@@ -334,7 +333,8 @@
         )
     stat = total / n_seg
     semi_ref[...] = stat.astype(semi_ref.dtype)
-    cols.wait_recv()
+    remote(lat_cols, lat_cols, cs_sem, cr_sem, (seg, lat_peers[1])).wait_recv()
+    col = psum[0]
     for j in range(1, n_lat):
         col = col + col_in[j]
     global_mean = (col / n_seg) / total_count
@@ -345,12 +345,7 @@
         mean = block_sum / jnp.full((1, width), cnt_ref[b], i32).astype(f32)
         excess_ref[b : b + 1, :] = mean - global_mean
 
-    cols.wait_send()
-
-    def sent(blocks, sem):
-        ref = far_rows.at[pl.ds(0, blocks)]
-        remote(ref, ref, sem, xr_sem.at[0], (seg_peers[1], lat)).wait_send()
-
+    sent(col_in.at[pl.ds(0, peers)], cs_sem)
     for q in range(PARTS):
         skipped = group * sum(owner == q for owner, _ in DIRECT)
         across = group // 2 * sum(owner ^ g == q for owner, g in DIRECT)
@@ -358,9 +353,8 @@
 
             @pl.when((quarter == q) & (parity == core))
             def _(skipped=skipped, across=across, core=core):
-                sent((n_seg - 1) * n_lat - (0 if core else skipped), xs_sem)
-                if across:
-                    sent(across, ds_sem)
+                count = n_seg * n_lat - 1 - (0 if core else skipped) + across
+                sent(far_rows.at[pl.ds(0, count)], rs_sem)
 
 
 def deliver(semi_ref, excess_ref, semi_out, excess_out, sem):
@@ -400,30 +394,24 @@
             pltpu.VMEM((1, points), jnp.int32),
             pltpu.SMEM((blocks,), jnp.int32),
             pltpu.VMEM((slice_bins, width), coh_map.dtype),
-            pltpu.VMEM((n_lat, 4, points), jnp.int32),
+            pltpu.VMEM((n_lat + n_seg, 4, points), jnp.int32),
             pltpu.VMEM((n_lat, slots, width), f32),
             pltpu.VMEM((n_lat, slots, width), f32),
             pltpu.VMEM((1, 1, width), f32),
-            pltpu.VMEM((n_lat, 1, width), f32),
-            pltpu.VMEM((n_seg, 4, points), jnp.int32),
-            pltpu.VMEM((n_seg * n_lat, slots, width), f32),
+            pltpu.VMEM((n_lat + n_seg, 1, width), f32),
+            pltpu.VMEM((n_seg * n_lat + n_lat // PARTS, slots, width), f32),
             pltpu.VMEM((1, 1, width), f32),
-            pltpu.VMEM((n_seg, 1, width), f32),
             dma,
             dma,
             dma((PARTS,)),
             dma,
-            dma((n_lat,)),
-            dma,
-            dma,
-            dma,
-            dma((PARTS,)),
-            dma,
-            dma,
+            dma((n_lat - 1,)),
+            dma,
+            dma,
+            dma((PARTS - 1,)),
             dma,
             dma,
             dma((2,)),
-            dma,
         ],
         compiler_params=pltpu.CompilerParams(collective_id=0, has_side_effects=True),
     )(positions, counts, coh_map)

time: 19.7 us -> 19.3 us (0.980)
  the two profiles are of different devices: /device:TPU:9 before, /device:TPU:0 now
where the time goes in v4:
time: 19.3 us; the launch traced here: 19.2 us
  Pallas kernels  18.5 us (96%)
  between operations  0.64 us (3%)
    pallas_call x1, Pallas kernels, shards(): pl.pallas_call(functools.partial(kernel, n_lat, n_seg), out_shape=(pltpu....  17.9 us
    pallas_call x1, Pallas kernels, shards(): pl.pallas_call(deliver, out_shape=tuple((jax.ShapeDtypeStruct(x.shape, x....  0.64 us

profile of v4, /device:TPU:0, one launch (start us, length us, event | category | flops | bytes accessed | tf_op | source)
XLA Modules:
  0.0 19.2 jit_solution(14740069126616825465)
XLA Ops:
  0.6 17.9 %shard_map.50 = (bf16[128,128]{1,0:T(8,128)(2,1)S(1)}, f32[2,128]{1,0:T(2,128)S(1)}) custom-call(s32[1,128]{1,0:T(1,128)} %pos_hbm.1, s32[2]{0:T(128)} %cnt_hbm.1, bf16[1,8192,128]{2,1,0:T(8,128)(2,1)} %coh_hbm.1), custom_call_target="tpu_custom_call" | custom-call | tf_op jit(solution)/shard_map/pallas_call | solution.py:378
  18.5 0.6 %shard_map.51 = (bf16[128,128]{1,0:T(8,128)(2,1)}, f32[2,128]{1,0:T(2,128)}) custom-call(bf16[128,128]{1,0:T(8,128)(2,1)S(1)} %get-tuple-element.4.semi_ref, f32[2,128]{1,0:T(2,128)S(1)} %get-tuple-element.5.excess_ref), custom_call_target="tpu_custom_call" | custom-call | tf_op jit(solution)/shard_map/pallas_call | solution.py:419

commit v5 on v4

--- a/solution.py
+++ b/solution.py
@@ -260,6 +260,11 @@
             makers = [owner ^ r for owner, r in DIRECT if turns[n][owner ^ r] == r]
             if makers:
                 pl.when(sum(is_quarter[q] for q in makers) == 1)(crosses[n])
+        if step == 1:
+            remote(
+                rows_out.at[1], rows_in.at[1], rs_sem, rr_sem.at[0], (seg, lat_peers[1])
+            ).wait_recv()
+            hand_on(rows_in.at[1], 1, 0)
         col = col + jnp.sum(jnp.where(kind > 1, held, 0.0), axis=0, keepdims=True)
     col_out[0] = col
     for m in seg_far_first:
@@ -287,13 +292,41 @@
         elif turn == 3:
             pl.when(jnp.logical_not(quarter >= 2))(seg_sum)
         first, peers = order(turns) if turn else (0, lat_peers[:group])
-        for i in range(group):
-            j = first + i
-            if turn or i:
+        def one_by_one(turn=turn, first=first, peers=peers):
+            for i in range(group):
+                j = first + i
+                if turn or i > 1:
+                    remote(
+                        rows_out.at[j], rows_in.at[j], rs_sem, rr_sem.at[j - 1], (seg, peers[i])
+                    ).wait_recv()
+                    hand_on(rows_in.at[j], j, first // group, turn)
+
+        def together(turn=turn, first=first, peers=peers):
+            for i in range(group):
                 remote(
-                    rows_out.at[j], rows_in.at[j], rs_sem, rr_sem.at[j - 1], (seg, peers[i])
+                    rows_out.at[0], rows_in.at[0], rs_sem, rr_sem.at[first + i - 1], (seg, peers[i])
                 ).wait_recv()
-                hand_on(rows_in.at[j], j, first // group, turn)
+            g = first // group
+            for m in seg_far_first:
+                copy = remote(
+                    rows_in.at[pl.ds(first, group)],
+                    far_rows.at[pl.ds(m * n_lat + first, group)],
+                    rs_sem,
+                    xr_sem.at[g - (g + PARTS - 1) // PARTS],
+                    (seg_peers[m], lat),
+                )
+                skips = [owner for owner, r in DIRECT if ARRIVE[turn][owner] == r]
+                if skips and m == n_seg - 1:
+                    pl.when(sum(is_quarter[owner] for owner in skips) == 0)(copy.start)
+                else:
+                    copy.start()
+
+        if turn in (2, 3):
+            whole = (parity == 0) & (quarter == 0)
+            pl.when(whole)(together)
+            pl.when(jnp.logical_not(whole))(one_by_one)
+        else:
+            one_by_one()
 
     theirs = gath.at[pl.ds(n_lat + 1, n_seg - 1)]
     remote(theirs, theirs, gs_sem, sr_sem, (seg_peers[1], lat)).wait_recv()

time: 19.3 us -> 19.2 us (level)
  no operation moved by 1% of the time
where the time goes in v5:
time: 19.2 us; the launch traced here: 19 us
  Pallas kernels  18.4 us (96%)
  between operations  0.64 us (3%)
    pallas_call x1, Pallas kernels, shards(): pl.pallas_call(functools.partial(kernel, n_lat, n_seg), out_shape=(pltpu....  17.8 us
    pallas_call x1, Pallas kernels, shards(): pl.pallas_call(deliver, out_shape=tuple((jax.ShapeDtypeStruct(x.shape, x....  0.64 us

profile of v5, /device:TPU:0, one launch (start us, length us, event | category | flops | bytes accessed | tf_op | source)
XLA Modules:
  0.0 19.0 jit_solution(12903743860277469699)
XLA Ops:
  0.6 17.8 %shard_map.50 = (bf16[128,128]{1,0:T(8,128)(2,1)S(1)}, f32[2,128]{1,0:T(2,128)S(1)}) custom-call(s32[1,128]{1,0:T(1,128)} %pos_hbm.1, s32[2]{0:T(128)} %cnt_hbm.1, bf16[1,8192,128]{2,1,0:T(8,128)(2,1)} %coh_hbm.1), custom_call_target="tpu_custom_call" | custom-call | tf_op jit(solution)/shard_map/pallas_call | solution.py:411
  18.4 0.6 %shard_map.51 = (bf16[128,128]{1,0:T(8,128)(2,1)}, f32[2,128]{1,0:T(2,128)}) custom-call(bf16[128,128]{1,0:T(8,128)(2,1)S(1)} %get-tuple-element.4.semi_ref, f32[2,128]{1,0:T(2,128)S(1)} %get-tuple-element.5.excess_ref), custom_call_target="tpu_custom_call" | custom-call | tf_op jit(solution)/shard_map/pallas_call | solution.py:452

commit v6 on v5

--- a/solution.py
+++ b/solution.py
@@ -131,7 +131,6 @@
     gath[0, 0:1, :] = sid
     gath[0, 1:2, :] = pos
     gath[0, 2:3, :] = valid
-    gath[0, 3:4, :] = valid
 
     straight = sum(is_quarter[owner ^ g] for owner, g in DIRECT)
     pl.semaphore_wait(barrier, n_lat - 1 + n_seg - 1 + straight * (group // 2))
@@ -427,7 +426,7 @@
             pltpu.VMEM((1, points), jnp.int32),
             pltpu.SMEM((blocks,), jnp.int32),
             pltpu.VMEM((slice_bins, width), coh_map.dtype),
-            pltpu.VMEM((n_lat + n_seg, 4, points), jnp.int32),
+            pltpu.VMEM((n_lat + n_seg, 3, points), jnp.int32),
             pltpu.VMEM((n_lat, slots, width), f32),
             pltpu.VMEM((n_lat, slots, width), f32),
             pltpu.VMEM((1, 1, width), f32),

time: 19.2 us -> 19.2 us (level)
  no operation moved by 1% of the time
where the time goes in v6:
time: 19.2 us; the launch traced here: 19 us
  Pallas kernels  18.4 us (96%)
  between operations  0.64 us (3%)
    pallas_call x1, Pallas kernels, shards(): pl.pallas_call(functools.partial(kernel, n_lat, n_seg), out_shape=(pltpu....  17.7 us
    pallas_call x1, Pallas kernels, shards(): pl.pallas_call(deliver, out_shape=tuple((jax.ShapeDtypeStruct(x.shape, x....  0.64 us

profile of v6, /device:TPU:0, one launch (start us, length us, event | category | flops | bytes accessed | tf_op | source)
XLA Modules:
  0.0 19.0 jit_solution(14985276719594453152)
XLA Ops:
  0.6 17.7 %shard_map.50 = (bf16[128,128]{1,0:T(8,128)(2,1)S(1)}, f32[2,128]{1,0:T(2,128)S(1)}) custom-call(s32[1,128]{1,0:T(1,128)} %pos_hbm.1, s32[2]{0:T(128)} %cnt_hbm.1, bf16[1,8192,128]{2,1,0:T(8,128)(2,1)} %coh_hbm.1), custom_call_target="tpu_custom_call" | custom-call | tf_op jit(solution)/shard_map/pallas_call | solution.py:410
  18.4 0.6 %shard_map.51 = (bf16[128,128]{1,0:T(8,128)(2,1)}, f32[2,128]{1,0:T(2,128)}) custom-call(bf16[128,128]{1,0:T(8,128)(2,1)S(1)} %get-tuple-element.4.semi_ref, f32[2,128]{1,0:T(2,128)S(1)} %get-tuple-element.5.excess_ref), custom_call_target="tpu_custom_call" | custom-call | tf_op jit(solution)/shard_map/pallas_call | solution.py:451
